TPU v7x, 128 devices: a whole 4x4x4 slice. The times are simulated.
128 devices in a mesh: replica: 1, data2: 2 (over core), data: 64 (over z, y, x).
Axes of the slice: x: 4, y: 4, z: 4, core: 2. Of those that a mesh axis runs over, the one named last changes fastest.
Arguments:
- query_hidden: bfloat16 [512, 32, 768], P(('replica', 'data2', 'data'))
- doc_hidden: bfloat16 [512, 180, 768], P(('replica', 'data2', 'data'))
- w_proj: bfloat16 [768, 128], replicated
- query_mask: int32 [512, 32], P(('replica', 'data2', 'data'))
- doc_mask: int32 [512, 180], P(('replica', 'data2', 'data'))
- temperature: float32 [], replicated
Outputs:
- output 1: float32 [512], P(('replica', 'data2', 'data'))
- output 2: float32 [1], P('replica')
All inputs are finite; a program needn't handle non-finite values.
Results may differ from a plain program's by a relative error of at most 0.001.
Values are sent between devices in bfloat16 or wider.
A program may use at most 1 GiB of HBM per device.

v0:
```python
import jax
import jax.numpy as jnp
from jax import lax
from jax.experimental import pallas as pl
from jax.experimental.pallas import tpu as pltpu
from jax.sharding import PartitionSpec as P

RING = 4
SLOT = 16
OTHERS = (1, 2, 3)


def unit_rows(hidden, w):
    projected = jnp.dot(hidden, w, preferred_element_type=jnp.float32)
    norm_len = jnp.sqrt(jnp.sum(projected * projected, axis=-1, keepdims=True))
    return projected / jnp.maximum(norm_len, 1e-12)


def as_column(row_mask, rows):
    r = lax.broadcasted_iota(jnp.int32, (rows, rows), 0)
    c = lax.broadcasted_iota(jnp.int32, (rows, rows), 1)
    return jnp.sum(jnp.where(r == c, row_mask, 0.0), axis=1, keepdims=True)


def make_kernel(n_docs, dlen, n_q, qlen):
    doc_rows = n_docs * dlen
    head = doc_rows // 2 // 16 * 16 + 16
    halves = (pl.ds(0, head), pl.ds(head, doc_rows - head))
    chunks = n_q * qlen // SLOT
    color_of = (pl.ds(0, chunks // 2), pl.ds(chunks // 2, chunks // 2))
    plane = RING * RING * SLOT
    n_dev = 2 * RING ** 3

    def kernel(qh_hbm, dh_hbm, w_hbm, qm_ref, dm_ref, temp_ref, loss_ref, mean_ref,
               qh, dh, w, qbuf, pbuf, pieces,
               load_sem, qsend, qrecv, zsend, zrecv, fsend, frecv, dsend, drecv, rsend, rrecv):
        core = lax.axis_index('data2')
        me = lax.axis_index('data')
        z, y, x = me // (RING * RING), (me // RING) % RING, me % RING

        def at(dz, dy, dx):
            return {'data': (((z + dz) % RING) * RING + (y + dy) % RING) * RING + (x + dx) % RING}

        sibling = {'data2': 1 - core}
        up, down = at(1, 0, 0), at(RING - 1, 0, 0)
        barrier = pltpu.get_barrier_semaphore()
        near = [at(0, 0, o) for o in OTHERS] + [at(0, o, 0) for o in OTHERS] + [sibling]
        near += [at(o, 0, 0) for o in OTHERS] + [at(o, 0, 0) | sibling for o in OTHERS]
        for device in near:
            pl.semaphore_signal(barrier, inc=1, device_id=device)

        loads = [pltpu.make_async_copy(src, dst, load_sem.at[i])
                 for i, (src, dst) in enumerate(((w_hbm, w), (qh_hbm, qh), (dh_hbm, dh)))]
        for load in loads:
            load.start()

        q_rows = n_q * qlen
        qm = qm_ref[...].astype(jnp.float32)
        q_keep = jnp.concatenate([as_column(qm[i:i + 1], qlen) for i in range(n_q)], axis=0)
        r = lax.broadcasted_iota(jnp.int32, (q_rows, q_rows), 0)
        c = lax.broadcasted_iota(jnp.int32, (q_rows, q_rows), 1)
        order = jnp.where(c == (r % n_q) * qlen + r // n_q, 1.0, 0.0).astype(jnp.bfloat16)
        loads[0].wait()
        loads[1].wait()
        w_val = w[...]
        q_unit = unit_rows(qh[...].reshape(q_rows, qh.shape[2]), w_val)
        q_vec = jnp.where(q_keep > 0, q_unit, 0.0).astype(jnp.bfloat16)
        q_ord = jnp.dot(order, q_vec, preferred_element_type=jnp.float32).astype(jnp.bfloat16)
        q_ord = q_ord.reshape(chunks, SLOT, q_ord.shape[1])
        for k in range(chunks):
            qbuf[k, y, x] = q_ord[k]

        def line_copy(color, phase, off):
            along_x = color == phase
            rows = y if along_x or phase == 0 else slice(None)
            cols = x if not along_x or phase == 0 else slice(None)
            if phase == 1:
                rows, cols = (y, slice(None)) if color == 0 else (slice(None), x)
            ref = qbuf.at[color_of[color], rows, cols]
            return pltpu.make_async_remote_copy(
                src_ref=ref, dst_ref=ref,
                send_sem=qsend.at[color, phase, off - 1], recv_sem=qrecv.at[color, phase, off - 1],
                device_id=at(0, 0, off) if along_x else at(0, off, 0))

        pl.semaphore_wait(barrier, len(near))
        for color in range(2):
            for off in OTHERS:
                line_copy(color, 0, off).start()

        dm = dm_ref[...].astype(jnp.float32)
        lane = lax.broadcasted_iota(jnp.int32, dm.shape, 1)
        first = jnp.min(jnp.where(dm > 0, lane, dlen), axis=1, keepdims=True)
        r = lax.broadcasted_iota(jnp.int32, (n_docs, doc_rows), 1)
        d = lax.broadcasted_iota(jnp.int32, (n_docs, doc_rows), 0)
        pick = jnp.where(r == first * n_docs + d, 1.0, 0.0).astype(jnp.bfloat16)
        r = lax.broadcasted_iota(jnp.int32, (doc_rows, dlen), 0)
        c = lax.broadcasted_iota(jnp.int32, (doc_rows, dlen), 1)
        spread = jnp.where(r // n_docs == c, 1.0, 0.0).astype(jnp.bfloat16)
        keep = lax.dot_general(spread, dm.astype(jnp.bfloat16), (((1,), (1,)), ((), ())),
                               preferred_element_type=jnp.float32)
        r = lax.broadcasted_iota(jnp.int32, keep.shape, 0)
        c = lax.broadcasted_iota(jnp.int32, keep.shape, 1)
        keep = jnp.sum(jnp.where(r % n_docs == c, keep, 0.0), axis=1, keepdims=True)
        loads[2].wait()
        unit = unit_rows(dh[...].reshape(doc_rows, dh.shape[2]), w_val)
        unit = jnp.where(keep > 0, unit, 0.0).astype(jnp.bfloat16)
        valid = jnp.dot(pick, unit, preferred_element_type=jnp.float32)
        valid = jnp.concatenate([valid, valid], axis=0)
        valid = jnp.broadcast_to(valid[None], (doc_rows // 8, 8, valid.shape[1]))
        filled = jnp.where(keep > 0, unit.astype(jnp.float32), valid.reshape(doc_rows, valid.shape[2]))
        pbuf[z, core] = filled.astype(jnp.bfloat16)

        def doc_part(rel, h):
            return pbuf.at[(z + rel) % RING, core, halves[h]]

        def swap_copy(rel, h):
            ref = doc_part(rel, h)
            return pltpu.make_async_remote_copy(
                src_ref=ref, dst_ref=ref, send_sem=dsend.at[rel, h], recv_sem=drecv.at[rel, h],
                device_id=sibling)

        def z_copy(way, h):
            ref = doc_part(0, h)
            return pltpu.make_async_remote_copy(
                src_ref=ref, dst_ref=ref, send_sem=zsend.at[way, h], recv_sem=zrecv.at[way, h],
                device_id=down if way else up)

        def pass_copy(way):
            ref = doc_part(1 if way else RING - 1, way)
            return pltpu.make_async_remote_copy(
                src_ref=ref, dst_ref=ref, send_sem=fsend.at[way], recv_sem=frecv.at[way],
                device_id=down if way else up)

        for i in range(2):
            for way in range(2):
                z_copy(way, way ^ i).start()
        for h in range(2):
            swap_copy(0, h).start()

        for color in range(2):
            for off in OTHERS:
                line_copy(color, 0, off).wait_recv()
            for off in OTHERS:
                line_copy(color, 1, off).start()

        sub = lax.broadcasted_iota(jnp.int32, (8, plane), 0)

        def score(rel, side):
            total = None
            for k in range(chunks):
                sim = lax.dot_general(pbuf[(z + rel) % RING, side], qbuf[k].reshape(plane, qbuf.shape[-1]),
                                      (((1,), (1,)), ((), ())), preferred_element_type=jnp.float32)
                best = jnp.max(sim.reshape(doc_rows // 8, 8, plane), axis=0)
                best = jnp.maximum(best, pltpu.roll(best, 4, 0))
                total = best if total is None else total + best
            return total

        got = {}
        for way in range(2):
            z_copy(way, way).wait_recv()
            pass_copy(way).start()
            swap_copy(1 if way else 3, way).start()
        for color in range(2):
            for off in OTHERS:
                line_copy(color, 1, off).wait_recv()
        got[0, 0] = score(0, core)
        for way in range(2):
            z_copy(way, 1 - way).wait_recv()
            swap_copy(1 if way else 3, 1 - way).start()
        for h in range(2):
            swap_copy(0, h).wait_recv()
        got[0, 1] = score(0, 1 - core)
        for rel in (3, 1):
            got[rel, 0] = score(rel, core)
        for way in range(2):
            pass_copy(way).wait_recv()
            swap_copy(2, way).start()
        for rel in (3, 1):
            for h in range(2):
                swap_copy(rel, h).wait_recv()
            got[rel, 1] = score(rel, 1 - core)
        got[2, 0] = score(2, core)
        for h in range(2):
            swap_copy(2, h).wait_recv()
        got[2, 1] = score(2, 1 - core)

        temp = temp_ref[0, 0]
        logits = []
        for rel in range(RING):
            s = jnp.where(sub < 4, got[rel, 0], got[rel, 1])
            s = s + pltpu.roll(s, n_q, 1)
            s = s + pltpu.roll(s, 2 * n_q, 1)
            logits.append(s / temp)
        peak = jnp.maximum(jnp.maximum(logits[0], logits[1]), jnp.maximum(logits[2], logits[3]))
        peak = jnp.max(peak, axis=0, keepdims=True)
        mass = sum(jnp.exp(g - peak) for g in logits)
        part = peak + jnp.log(jnp.sum(mass, axis=0, keepdims=True))
        lanes = lax.broadcasted_iota(jnp.int32, (8, plane), 1)
        is_own = (sub == lanes % n_q) & (lanes // SLOT == y * RING + x) & (lanes % SLOT >= SLOT - n_q)
        own = jnp.sum(jnp.where(is_own, logits[0], 0.0), axis=0, keepdims=True)
        own_sum = jnp.sum(own, axis=1, keepdims=True)
        slot = lax.broadcasted_iota(jnp.int32, (1, 128), 1) % SLOT

        def fold(row):
            return jnp.where(slot >= 12, row[:, :128], pltpu.roll(row[:, 128:], 128 - n_q, 1))

        row = jnp.where(slot >= 8, fold(part), own_sum)
        own = fold(own)
        here = core * RING ** 3 + me
        pieces[here] = row

        def tell(step):
            other = {'data2': (core + step // RING ** 3) % 2, 'data': (me + step) % RING ** 3}
            return pltpu.make_async_remote_copy(
                src_ref=pieces.at[here], dst_ref=pieces.at[here], send_sem=rsend, recv_sem=rrecv,
                device_id=other)

        for step in range(1, n_dev):
            tell(step).start()
        everyone = pieces.at[pl.ds(0, n_dev - 1)]
        pltpu.make_async_copy(everyone, everyone, rrecv).wait()
        total = jnp.zeros((1, 1), jnp.float32)
        losses = jnp.zeros((1, 128), jnp.float32)
        for group in range(2 * RING):
            ls = [pieces[group * RING * RING + i] for i in range(RING * RING)]
            peak = ls[0]
            for l in ls[1:]:
                peak = jnp.maximum(peak, l)
            mass = sum(jnp.exp(l - peak) for l in ls)
            whole = peak + jnp.log(mass)
            total = total + jnp.sum(jnp.where(slot >= 8, whole, 0.0), axis=1, keepdims=True)
            total = total - sum(ls)[:, 0:1]
            losses = jnp.where(group == core * RING + z, whole, losses)
        losses = losses - own
        spot = (y * RING + x) % 8 * SLOT + jnp.where(y >= 2, 8, 12)
        losses = pltpu.roll(jnp.broadcast_to(losses, (8, 128)), (128 - spot) % 128, 1)
        loss_ref[...] = losses[0:1, :n_q]
        mean_ref[...] = total / (n_dev * n_q)

        for color in range(2):
            for phase in range(2):
                for off in OTHERS:
                    line_copy(color, phase, off).wait_send()
        for way in range(2):
            for h in range(2):
                z_copy(way, h).wait_send()
            pass_copy(way).wait_send()
        for rel in range(RING):
            for h in range(2):
                swap_copy(rel, h).wait_send()
        pltpu.make_async_copy(everyone, everyone, rsend).wait()

    return kernel


def solution(mesh):
    row_spec = P(('replica', 'data2', 'data'))
    tok_spec = P(('replica', 'data2', 'data'), None, None)
    mask_spec = P(('replica', 'data2', 'data'), None)

    def local_step(query_hidden, doc_hidden, w_proj, query_mask, doc_mask, temperature):
        n_q, qlen, hidden = query_hidden.shape
        n_docs, dlen, _ = doc_hidden.shape
        proj = w_proj.shape[1]
        chunks = n_q * qlen // SLOT
        dma = pltpu.SemaphoreType.DMA
        losses, mean = pl.pallas_call(
            make_kernel(n_docs, dlen, n_q, qlen),
            out_shape=(jax.ShapeDtypeStruct((1, n_q), jnp.float32),
                       jax.ShapeDtypeStruct((1, 1), jnp.float32)),
            in_specs=[pl.BlockSpec(memory_space=pl.ANY)] * 3
            + [pl.BlockSpec(memory_space=pltpu.VMEM)] * 2
            + [pl.BlockSpec(memory_space=pltpu.SMEM)],
            out_specs=(pl.BlockSpec(memory_space=pltpu.VMEM), pl.BlockSpec(memory_space=pltpu.VMEM)),
            scratch_shapes=[
                pltpu.VMEM(query_hidden.shape, jnp.bfloat16),
                pltpu.VMEM((dlen, n_docs, hidden), jnp.bfloat16),
                pltpu.VMEM(w_proj.shape, jnp.bfloat16),
                pltpu.VMEM((chunks, RING, RING, SLOT, proj), jnp.bfloat16),
                pltpu.VMEM((RING, 2, n_docs * dlen, proj), jnp.bfloat16),
                pltpu.VMEM((2 * RING ** 3, 1, 128), jnp.float32),
                dma((3,)),
                dma((2, 2, 3)), dma((2, 2, 3)),
                dma((2, 2)), dma((2, 2)),
                dma((2,)), dma((2,)),
                dma((RING, 2)), dma((RING, 2)),
                dma, dma,
            ],
            compiler_params=pltpu.CompilerParams(collective_id=0, has_side_effects=True),
        )(query_hidden, jnp.transpose(doc_hidden, (1, 0, 2)), w_proj, query_mask, doc_mask,
          temperature.reshape(1, 1))
        return losses.reshape(n_q), mean.reshape(1)

    return jax.shard_map(local_step, mesh=mesh,
                         in_specs=(tok_spec, tok_spec, P(None, None), mask_spec, mask_spec, P()),
                         out_specs=(row_spec, P('replica')), check_vma=False)
```

profile of v0, /device:TPU:1, one launch (start us, length us, event | category | flops | bytes accessed | tf_op | source)
XLA Modules:
  0.0 35.7 jit_solution(3946862127655410760)
XLA Ops:
  1.3 31.6 %shard_map.77 = (f32[1,4]{1,0:T(1,128)}, f32[1,1]{1,0:T(1,128)}) custom-call(bf16[4,32,768]{2,1,0:T(8,128)(2,1)} %qh_hbm.1, bf16[180,4,768]{2,1,0:T(4,128)(2,1)} %bitcast.5, bf16[768,128]{1,0:T(8,128)(2,1)} %w_hbm.1, s32[4,32]{1,0:T(4,128)} %qm_ref.1, s32[4,180]{1,0:T(4,128)} %dm_ref.1, f32[1,1]{1,0:T(1,128)} %bitcast.4.temp_ref), custom_call_target="tpu_custom_call" | custom-call | tf_op jit(solution)/shard_map/pallas_call | solution.py:267
  32.8 1.1 %copy.11 = f32[4]{0:T(128)} copy(f32[4]{0:T(128)} %bitcast.6) | data formatting | bytes 32
where the time goes:
time: 35.9 us; the launch traced here: 35.7 us
  Pallas kernels  31.6 us (88%)
  between operations  3.05 us (8%)
  local copies, waits for them, and re-layouts  1.11 us (3%)
    pallas_call x1, Pallas kernels, local_step(): pl.pallas_call(make_kernel(n_docs, dlen, n_q, qlen), out_shape=(jax.Shape...  31.6 us
    unnamed x1, local copies, waits for them, and re-layouts  1.11 us

commit v1 on v0

--- a/solution.py
+++ b/solution.py
@@ -22,12 +22,17 @@
     return jnp.sum(jnp.where(r == c, row_mask, 0.0), axis=1, keepdims=True)
 
 
+def far(*offsets):
+    return sum(min(o, RING - o) for o in offsets)
+
+
 def make_kernel(n_docs, dlen, n_q, qlen):
     doc_rows = n_docs * dlen
     head = doc_rows // 2 // 16 * 16 + 16
     halves = (pl.ds(0, head), pl.ds(head, doc_rows - head))
     chunks = n_q * qlen // SLOT
-    color_of = (pl.ds(0, chunks // 2), pl.ds(chunks // 2, chunks // 2))
+    steps = 4
+    per_step = chunks // steps
     plane = RING * RING * SLOT
     n_dev = 2 * RING ** 3
 
@@ -38,13 +43,19 @@
         me = lax.axis_index('data')
         z, y, x = me // (RING * RING), (me // RING) % RING, me % RING
 
+        zs = [(z + i) % RING * RING * RING for i in range(RING)]
+        ys = [(y + i) % RING * RING for i in range(RING)]
+        xs = [(x + i) % RING for i in range(RING)]
+
         def at(dz, dy, dx):
-            return {'data': (((z + dz) % RING) * RING + (y + dy) % RING) * RING + (x + dx) % RING}
+            return {'data': zs[dz] + ys[dy] + xs[dx]}
 
         sibling = {'data2': 1 - core}
         up, down = at(1, 0, 0), at(RING - 1, 0, 0)
         barrier = pltpu.get_barrier_semaphore()
-        near = [at(0, 0, o) for o in OTHERS] + [at(0, o, 0) for o in OTHERS] + [sibling]
+        mates = [(dy, dx) for dy in range(RING) for dx in range(RING) if dy or dx]
+        mates.sort(key=lambda m: -far(0, *m))
+        near = [at(0, *m) for m in mates] + [sibling]
         near += [at(o, 0, 0) for o in OTHERS] + [at(o, 0, 0) | sibling for o in OTHERS]
         for device in near:
             pl.semaphore_signal(barrier, inc=1, device_id=device)
@@ -70,22 +81,20 @@
         for k in range(chunks):
             qbuf[k, y, x] = q_ord[k]
 
-        def line_copy(color, phase, off):
-            along_x = color == phase
-            rows = y if along_x or phase == 0 else slice(None)
-            cols = x if not along_x or phase == 0 else slice(None)
-            if phase == 1:
-                rows, cols = (y, slice(None)) if color == 0 else (slice(None), x)
-            ref = qbuf.at[color_of[color], rows, cols]
-            return pltpu.make_async_remote_copy(
-                src_ref=ref, dst_ref=ref,
-                send_sem=qsend.at[color, phase, off - 1], recv_sem=qrecv.at[color, phase, off - 1],
-                device_id=at(0, 0, off) if along_x else at(0, off, 0))
+        def query_copy(step, mate):
+            ref = qbuf.at[pl.ds(step * per_step, per_step), y, x]
+            return pltpu.make_async_remote_copy(
+                src_ref=ref, dst_ref=ref, send_sem=qsend.at[step], recv_sem=qrecv.at[step],
+                device_id=at(0, *mate))
+
+        def query_wait(step, sem):
+            ref = qbuf.at[pl.ds(0, 5), pl.ds(0, 3), pl.ds(0, per_step)]
+            pltpu.make_async_copy(ref, ref, sem.at[step]).wait()
 
         pl.semaphore_wait(barrier, len(near))
-        for color in range(2):
-            for off in OTHERS:
-                line_copy(color, 0, off).start()
+        for step in range(steps):
+            for mate in mates:
+                query_copy(step, mate).start()
 
         dm = dm_ref[...].astype(jnp.float32)
         lane = lax.broadcasted_iota(jnp.int32, dm.shape, 1)
@@ -137,57 +146,63 @@
         for h in range(2):
             swap_copy(0, h).start()
 
-        for color in range(2):
-            for off in OTHERS:
-                line_copy(color, 0, off).wait_recv()
-            for off in OTHERS:
-                line_copy(color, 1, off).start()
-
         sub = lax.broadcasted_iota(jnp.int32, (8, plane), 0)
 
-        def score(rel, side):
-            total = None
-            for k in range(chunks):
-                sim = lax.dot_general(pbuf[(z + rel) % RING, side], qbuf[k].reshape(plane, qbuf.shape[-1]),
-                                      (((1,), (1,)), ((), ())), preferred_element_type=jnp.float32)
-                best = jnp.max(sim.reshape(doc_rows // 8, 8, plane), axis=0)
-                best = jnp.maximum(best, pltpu.roll(best, 4, 0))
-                total = best if total is None else total + best
-            return total
-
-        got = {}
+        total = {}
+
+        def score(rel, swapped, *which):
+            docs = pbuf[(z + rel) % RING, 1 - core if swapped else core]
+            for step in which:
+                for k in range(step * per_step, (step + 1) * per_step):
+                    sim = lax.dot_general(docs, qbuf[k].reshape(plane, qbuf.shape[-1]),
+                                          (((1,), (1,)), ((), ())), preferred_element_type=jnp.float32)
+                    best = jnp.max(sim.reshape(doc_rows // 8, 8, plane), axis=0)
+                    best = jnp.maximum(best, pltpu.roll(best, 4, 0))
+                    key = rel, swapped
+                    total[key] = total[key] + best if key in total else best
+
+        query_wait(0, qrecv)
         for way in range(2):
             z_copy(way, way).wait_recv()
             pass_copy(way).start()
             swap_copy(1 if way else 3, way).start()
-        for color in range(2):
-            for off in OTHERS:
-                line_copy(color, 1, off).wait_recv()
-        got[0, 0] = score(0, core)
+        score(0, 0, 0)
+        for h in range(2):
+            swap_copy(0, h).wait_recv()
+        score(0, 1, 0)
+        query_wait(1, qrecv)
+        score(0, 0, 1)
+        score(0, 1, 1)
         for way in range(2):
             z_copy(way, 1 - way).wait_recv()
             swap_copy(1 if way else 3, 1 - way).start()
-        for h in range(2):
-            swap_copy(0, h).wait_recv()
-        got[0, 1] = score(0, 1 - core)
-        for rel in (3, 1):
-            got[rel, 0] = score(rel, core)
+        score(3, 0, 0, 1)
+        score(1, 0, 0, 1)
+        query_wait(2, qrecv)
+        score(0, 0, 2)
+        score(0, 1, 2)
+        score(3, 0, 2)
+        score(1, 0, 2)
         for way in range(2):
             pass_copy(way).wait_recv()
             swap_copy(2, way).start()
         for rel in (3, 1):
             for h in range(2):
                 swap_copy(rel, h).wait_recv()
-            got[rel, 1] = score(rel, 1 - core)
-        got[2, 0] = score(2, core)
+            score(rel, 1, 0, 1, 2)
+        query_wait(3, qrecv)
+        for rel in (0, 3, 1):
+            score(rel, 0, 3)
+            score(rel, 1, 3)
+        score(2, 0, 0, 1, 2, 3)
         for h in range(2):
             swap_copy(2, h).wait_recv()
-        got[2, 1] = score(2, 1 - core)
+        score(2, 1, 0, 1, 2, 3)
 
         temp = temp_ref[0, 0]
         logits = []
         for rel in range(RING):
-            s = jnp.where(sub < 4, got[rel, 0], got[rel, 1])
+            s = jnp.where(sub < 4, total[rel, 0], total[rel, 1])
             s = s + pltpu.roll(s, n_q, 1)
             s = s + pltpu.roll(s, 2 * n_q, 1)
             logits.append(s / temp)
@@ -209,17 +224,18 @@
         here = core * RING ** 3 + me
         pieces[here] = row
 
-        def tell(step):
-            other = {'data2': (core + step // RING ** 3) % 2, 'data': (me + step) % RING ** 3}
+        def tell(across, dz, dy, dx):
+            other = at(dz, dy, dx) | {'data2': 1 - core if across else core}
             return pltpu.make_async_remote_copy(
                 src_ref=pieces.at[here], dst_ref=pieces.at[here], send_sem=rsend, recv_sem=rrecv,
                 device_id=other)
 
-        for step in range(1, n_dev):
-            tell(step).start()
+        rest = [(a, i, j, k) for a in range(2) for i in range(RING) for j in range(RING) for k in range(RING)]
+        for a, i, j, k in sorted(rest[1:], key=lambda o: -far(*o[1:])):
+            tell(a, i, j, k).start()
         everyone = pieces.at[pl.ds(0, n_dev - 1)]
         pltpu.make_async_copy(everyone, everyone, rrecv).wait()
-        total = jnp.zeros((1, 1), jnp.float32)
+        answer = jnp.zeros((1, 1), jnp.float32)
         losses = jnp.zeros((1, 128), jnp.float32)
         for group in range(2 * RING):
             ls = [pieces[group * RING * RING + i] for i in range(RING * RING)]
@@ -228,19 +244,17 @@
                 peak = jnp.maximum(peak, l)
             mass = sum(jnp.exp(l - peak) for l in ls)
             whole = peak + jnp.log(mass)
-            total = total + jnp.sum(jnp.where(slot >= 8, whole, 0.0), axis=1, keepdims=True)
-            total = total - sum(ls)[:, 0:1]
+            answer = answer + jnp.sum(jnp.where(slot >= 8, whole, 0.0), axis=1, keepdims=True)
+            answer = answer - sum(ls)[:, 0:1]
             losses = jnp.where(group == core * RING + z, whole, losses)
         losses = losses - own
         spot = (y * RING + x) % 8 * SLOT + jnp.where(y >= 2, 8, 12)
         losses = pltpu.roll(jnp.broadcast_to(losses, (8, 128)), (128 - spot) % 128, 1)
         loss_ref[...] = losses[0:1, :n_q]
-        mean_ref[...] = total / (n_dev * n_q)
-
-        for color in range(2):
-            for phase in range(2):
-                for off in OTHERS:
-                    line_copy(color, phase, off).wait_send()
+        mean_ref[...] = answer / (n_dev * n_q)
+
+        for step in range(steps):
+            query_wait(step, qsend)
         for way in range(2):
             for h in range(2):
                 z_copy(way, h).wait_send()
@@ -251,6 +265,11 @@
         pltpu.make_async_copy(everyone, everyone, rsend).wait()
 
     return kernel
+
+
+def hand_over(loss_in, mean_in, loss_ref, mean_ref):
+    loss_ref[...] = loss_in[...]
+    mean_ref[...] = mean_in[...]
 
 
 def solution(mesh):
@@ -280,7 +299,7 @@
                 pltpu.VMEM((RING, 2, n_docs * dlen, proj), jnp.bfloat16),
                 pltpu.VMEM((2 * RING ** 3, 1, 128), jnp.float32),
                 dma((3,)),
-                dma((2, 2, 3)), dma((2, 2, 3)),
+                dma((4,)), dma((4,)),
                 dma((2, 2)), dma((2, 2)),
                 dma((2,)), dma((2,)),
                 dma((RING, 2)), dma((RING, 2)),
@@ -289,6 +308,10 @@
             compiler_params=pltpu.CompilerParams(collective_id=0, has_side_effects=True),
         )(query_hidden, jnp.transpose(doc_hidden, (1, 0, 2)), w_proj, query_mask, doc_mask,
           temperature.reshape(1, 1))
+        losses, mean = pl.pallas_call(
+            hand_over,
+            out_shape=(jax.ShapeDtypeStruct((1, n_q), jnp.float32),
+                       jax.ShapeDtypeStruct((1, 1), jnp.float32)))(losses, mean)
         return losses.reshape(n_q), mean.reshape(1)
 
     return jax.shard_map(local_step, mesh=mesh,

time: 35.9 us -> 34.6 us (0.964)
  between operations: 3.05 us -> 1.29 us
  Pallas kernels: 31.6 us -> 33.1 us
  local copies, waits for them, and re-layouts: 1.11 us -> 0 us
    pallas_call x0 -> x1, Pallas kernels: none -> 1.78 us  [local_step(): pl.pallas_call(hand_over, out_shape=(jax.ShapeDtypeStruct((1, n_q), jnp.f...]
    unnamed x1 -> x0, local copies, waits for them, and re-layouts: 1.11 us -> none
where the time goes in v1:
time: 34.6 us; the launch traced here: 34.4 us
  Pallas kernels  33.1 us (96%)
  between operations  1.29 us (4%)
    pallas_call x1, Pallas kernels, local_step(): pl.pallas_call(make_kernel(n_docs, dlen, n_q, qlen), out_shape=(jax.Shape...  31.3 us
    pallas_call x1, Pallas kernels, local_step(): pl.pallas_call(hand_over, out_shape=(jax.ShapeDtypeStruct((1, n_q), jnp.f...  1.78 us

profile of v1, /device:TPU:1, one launch (start us, length us, event | category | flops | bytes accessed | tf_op | source)
XLA Modules:
  0.0 34.4 jit_solution(15736010207867053679)
XLA Ops:
  1.3 31.3 %shard_map.77 = (f32[1,4]{1,0:T(1,128)}, f32[1,1]{1,0:T(1,128)}) custom-call(bf16[4,32,768]{2,1,0:T(8,128)(2,1)} %qh_hbm.1, bf16[180,4,768]{2,1,0:T(4,128)(2,1)} %bitcast.5, bf16[768,128]{1,0:T(8,128)(2,1)} %w_hbm.1, s32[4,32]{1,0:T(4,128)} %qm_ref.1, s32[4,180]{1,0:T(4,128)} %dm_ref.1, f32[1,1]{1,0:T(1,128)} %bitcast.4.temp_ref), custom_call_target="tpu_custom_call" | custom-call | tf_op jit(solution)/shard_map/pallas_call | solution.py:286
  32.6 1.8 %shard_map.78 = (f32[1,4]{1,0:T(1,128)}, f32[1,1]{1,0:T(1,128)}) custom-call(f32[1,4]{1,0:T(1,128)} %get-tuple-element.6.loss_in, f32[1,1]{1,0:T(1,128)} %get-tuple-element.7.mean_in), custom_call_target="tpu_custom_call" | custom-call | tf_op jit(solution)/shard_map/pallas_call | solution.py:311

commit v2 on v1

v2 whole, which is shorter than its diff:
```python
import jax
import jax.numpy as jnp
from jax import lax
from jax.experimental import pallas as pl
from jax.experimental.pallas import tpu as pltpu
from jax.sharding import PartitionSpec as P

RING = 4
SLOT = 16
OTHERS = (1, 2, 3)


def unit_rows(hidden, w):
    projected = jnp.dot(hidden, w, preferred_element_type=jnp.float32)
    norm_len = jnp.sqrt(jnp.sum(projected * projected, axis=-1, keepdims=True))
    return projected / jnp.maximum(norm_len, 1e-12)


def as_column(row_mask, rows):
    r = lax.broadcasted_iota(jnp.int32, (rows, rows), 0)
    c = lax.broadcasted_iota(jnp.int32, (rows, rows), 1)
    return jnp.sum(jnp.where(r == c, row_mask, 0.0), axis=1, keepdims=True)


def far(*offsets):
    return sum(min(o, RING - o) for o in offsets)


def make_kernel(n_docs, dlen, n_q, qlen):
    doc_rows = n_docs * dlen
    head = doc_rows // 2 // 16 * 16 + 16
    parts = (pl.ds(0, head), pl.ds(head, doc_rows - head), pl.ds(0, doc_rows))
    chunks = n_q * qlen // SLOT
    tiles = chunks // RING
    rounds = 4
    plane = RING * RING * SLOT
    n_dev = 2 * RING ** 3

    def kernel(qh_hbm, dh_hbm, w_hbm, qm_hbm, dm_hbm, temp_hbm, out_ref,
               qh, dh, w, qm_ref, dm_ref, temp_ref, qbuf, pbuf, sums, pieces,
               load_sem, qsend, qrecv, zsend, zrecv, fsend, frecv, dsend, drecv, rsend, rrecv):
        loads = [pltpu.make_async_copy(src, dst, load_sem.at[i]) for i, (src, dst) in enumerate((
            (w_hbm, w), (qh_hbm, qh), (qm_hbm, qm_ref), (dm_hbm, dm_ref), (dh_hbm, dh),
            (temp_hbm, temp_ref)))]
        for load in loads:
            load.start()

        core = lax.axis_index('data2')
        me = lax.axis_index('data')
        z, y, x = me // (RING * RING), (me // RING) % RING, me % RING

        zs = [(z + i) % RING * RING * RING for i in range(RING)]
        ys = [(y + i) % RING * RING for i in range(RING)]
        xs = [(x + i) % RING for i in range(RING)]

        def at(dz, dy, dx):
            return {'data': zs[dz] + ys[dy] + xs[dx]}

        sibling = {'data2': 1 - core}
        up, down = at(1, 0, 0), at(RING - 1, 0, 0)
        barrier = pltpu.get_barrier_semaphore()
        mates = [(dy, dx) for dy in range(RING) for dx in range(RING) if dy or dx]
        mates.sort(key=lambda m: (far(m[0]), -far(m[1])))
        near = [at(0, *m) for m in mates] + [sibling]
        near += [at(o, 0, 0) for o in OTHERS] + [at(o, 0, 0) | sibling for o in OTHERS]
        for device in near:
            pl.semaphore_signal(barrier, inc=1, device_id=device)

        q_rows = n_q * qlen
        r = lax.broadcasted_iota(jnp.int32, (q_rows, q_rows), 0)
        c = lax.broadcasted_iota(jnp.int32, (q_rows, q_rows), 1)
        order = jnp.where(c == (r % n_q) * qlen + r // n_q, 1.0, 0.0).astype(jnp.bfloat16)
        r = lax.broadcasted_iota(jnp.int32, (doc_rows, dlen), 0)
        c = lax.broadcasted_iota(jnp.int32, (doc_rows, dlen), 1)
        spread = jnp.where(r // n_docs == c, 1.0, 0.0).astype(jnp.bfloat16)
        loads[2].wait()
        qm = qm_ref[...].astype(jnp.float32)
        q_keep = jnp.concatenate([as_column(qm[i:i + 1], qlen) for i in range(n_q)], axis=0)

        loads[0].wait()
        loads[1].wait()
        w_val = w[...]
        q_unit = unit_rows(qh[...].reshape(q_rows, qh.shape[2]), w_val)
        q_vec = jnp.where(q_keep > 0, q_unit, 0.0).astype(jnp.bfloat16)
        q_ord = jnp.dot(order, q_vec, preferred_element_type=jnp.float32).astype(jnp.bfloat16)
        q_ord = q_ord.reshape(chunks, SLOT, q_ord.shape[1])
        for k in range(chunks):
            qbuf[k, y, x] = q_ord[k]

        def query_copy(mate, rnd):
            ref = qbuf.at[pl.ds(rnd * (chunks // rounds), chunks // rounds), y, x]
            return pltpu.make_async_remote_copy(
                src_ref=ref, dst_ref=ref, send_sem=qsend.at[mate[0]], recv_sem=qrecv.at[mate[0]],
                device_id=at(0, *mate))

        def query_wait(dy, sem):
            ref = qbuf.at[:, (y + RING - dy) % RING, pl.ds(0, RING if dy else RING - 1)]
            pltpu.make_async_copy(ref, ref, sem.at[dy]).wait()

        pl.semaphore_wait(barrier, len(near))
        for near_row in (0, 1, 2):
            for rnd in range(rounds):
                for mate in mates:
                    if far(mate[0]) == near_row:
                        query_copy(mate, rnd).start()

        loads[3].wait()
        loads[4].wait()
        dm = dm_ref[...].astype(jnp.float32)
        lane = lax.broadcasted_iota(jnp.int32, dm.shape, 1)
        first = jnp.min(jnp.where(dm > 0, lane, dlen), axis=1, keepdims=True)
        r = lax.broadcasted_iota(jnp.int32, (n_docs, doc_rows), 1)
        d = lax.broadcasted_iota(jnp.int32, (n_docs, doc_rows), 0)
        pick = jnp.where(r == first * n_docs + d, 1.0, 0.0).astype(jnp.bfloat16)
        keep = lax.dot_general(spread, dm.astype(jnp.bfloat16), (((1,), (1,)), ((), ())),
                               preferred_element_type=jnp.float32)
        r = lax.broadcasted_iota(jnp.int32, keep.shape, 0)
        c = lax.broadcasted_iota(jnp.int32, keep.shape, 1)
        keep = jnp.sum(jnp.where(r % n_docs == c, keep, 0.0), axis=1, keepdims=True)
        unit = unit_rows(dh[...].reshape(doc_rows, dh.shape[2]), w_val)
        unit = jnp.where(keep > 0, unit, 0.0).astype(jnp.bfloat16)
        valid = jnp.dot(pick, unit, preferred_element_type=jnp.float32)
        valid = jnp.concatenate([valid, valid], axis=0)
        valid = jnp.broadcast_to(valid[None], (doc_rows // 8, 8, valid.shape[1]))
        filled = jnp.where(keep > 0, unit.astype(jnp.float32), valid.reshape(doc_rows, valid.shape[2]))
        pbuf[z, core] = filled.astype(jnp.bfloat16)

        def doc_part(rel, h):
            return pbuf.at[(z + rel) % RING, core, parts[h]]

        def swap_copy(rel, h):
            ref = doc_part(rel, h)
            return pltpu.make_async_remote_copy(
                src_ref=ref, dst_ref=ref, send_sem=dsend.at[rel, h % 2], recv_sem=drecv.at[rel, h % 2],
                device_id=sibling)

        def z_copy(way, h):
            ref = doc_part(0, h)
            return pltpu.make_async_remote_copy(
                src_ref=ref, dst_ref=ref, send_sem=zsend.at[way, h], recv_sem=zrecv.at[way, h],
                device_id=down if way else up)

        def pass_copy(way):
            ref = doc_part(1 if way else RING - 1, way)
            return pltpu.make_async_remote_copy(
                src_ref=ref, dst_ref=ref, send_sem=fsend.at[way], recv_sem=frecv.at[way],
                device_id=down if way else up)

        for i in range(2):
            for way in range(2):
                z_copy(way, way ^ i).start()
        swap_copy(0, 2).start()

        sub = lax.broadcasted_iota(jnp.int32, (8, plane), 0)
        found, total = {}, {}

        def score(rel, swapped, part, rows):
            docs = pbuf[(z + rel) % RING, 1 - core if swapped else core, parts[part]]
            for dy in rows:
                for t in range(tiles):
                    q_tile = qbuf[t * RING:(t + 1) * RING, (y + RING - dy) % RING].reshape(plane, qbuf.shape[-1])
                    sim = lax.dot_general(docs, q_tile, (((1,), (1,)), ((), ())),
                                          preferred_element_type=jnp.float32)
                    best = jnp.max(sim.reshape(docs.shape[0] // 8, 8, plane), axis=0)
                    tile, key = (rel, swapped, dy, t), (rel, swapped, dy)
                    if part < 2 and tile not in found:
                        found[tile] = best
                        continue
                    if part < 2:
                        best = jnp.maximum(best, found[tile])
                    best = jnp.maximum(best, pltpu.roll(best, 4, 0))
                    total[key] = total[key] + best if key in total else best

        every, early = (0, 1, 2, 3), (0, 1)
        query_wait(0, qrecv)
        swap_copy(0, 2).wait_recv()
        score(0, 0, 2, (0,))
        score(0, 1, 2, (0,))
        for way in range(2):
            z_copy(way, way).wait_recv()
            pass_copy(way).start()
            swap_copy(1 if way else 3, way).start()
        score(3, 0, 0, (0,))
        score(1, 0, 1, (0,))
        query_wait(1, qrecv)
        score(0, 0, 2, (1,))
        score(0, 1, 2, (1,))
        score(3, 0, 0, (1,))
        score(1, 0, 1, (1,))
        for way in range(2):
            z_copy(way, 1 - way).wait_recv()
            swap_copy(1 if way else 3, 1 - way).start()
        for way in range(2):
            swap_copy(1 if way else 3, way).wait_recv()
        score(3, 1, 0, early)
        score(1, 1, 1, early)
        query_wait(3, qrecv)
        score(0, 0, 2, (3,))
        score(0, 1, 2, (3,))
        score(3, 0, 0, (3,))
        score(1, 0, 1, (3,))
        score(3, 1, 0, (3,))
        score(1, 1, 1, (3,))
        score(3, 0, 1, (0, 1, 3))
        score(1, 0, 0, (0, 1, 3))
        for way in range(2):
            pass_copy(way).wait_recv()
            swap_copy(2, way).start()
        query_wait(2, qrecv)
        for way in range(2):
            swap_copy(1 if way else 3, 1 - way).wait_recv()
        score(0, 0, 2, (2,))
        score(0, 1, 2, (2,))
        for way in range(2):
            rel = 1 if way else 3
            score(rel, 0, way, (2,))
            score(rel, 1, way, (2,))
            score(rel, 0, 1 - way, (2,))
            score(rel, 1, 1 - way, every)
        score(2, 0, 2, every)
        for h in range(2):
            swap_copy(2, h).wait_recv()
        score(2, 1, 2, every)

        half = lax.broadcasted_iota(jnp.int32, (8, 128), 1) < 64
        for rel in range(RING):
            for dy in range(RING):
                s = jnp.where(sub < 4, total[rel, 0, dy], total[rel, 1, dy])
                s = s[:, :128] + s[:, 128:]
                sums[rel, (y + RING - dy) % RING] = s + pltpu.roll(s, 64, 1)
        loads[5].wait()
        temp = temp_ref[...]
        logits = []
        for rel in range(RING):
            s = jnp.concatenate([jnp.where(half, sums[rel, i], sums[rel, i + 1]) for i in (0, 2)], axis=1)
            s = s + pltpu.roll(s, n_q, 1)
            s = s + pltpu.roll(s, 2 * n_q, 1)
            logits.append(s / temp)
        peak = jnp.maximum(jnp.maximum(logits[0], logits[1]), jnp.maximum(logits[2], logits[3]))
        peak = jnp.max(peak, axis=0, keepdims=True)
        mass = sum(jnp.exp(g - peak) for g in logits)
        part = peak + jnp.log(jnp.sum(mass, axis=0, keepdims=True))
        lanes = lax.broadcasted_iota(jnp.int32, (8, plane), 1)
        is_own = (sub == lanes % n_q) & (lanes // SLOT == y * RING + x) & (lanes % SLOT >= SLOT - n_q)
        own = jnp.sum(jnp.where(is_own, logits[0], 0.0), axis=0, keepdims=True)
        own_sum = jnp.sum(own, axis=1, keepdims=True)
        slot = lax.broadcasted_iota(jnp.int32, (1, 128), 1) % SLOT

        def fold(row):
            return jnp.where(slot >= 12, row[:, :128], pltpu.roll(row[:, 128:], 128 - n_q, 1))

        row = jnp.where(slot >= 8, fold(part), own_sum)
        own = fold(own)
        here = core * RING ** 3 + me
        pieces[here] = row

        def tell(across, dz, dy, dx):
            other = at(dz, dy, dx) | {'data2': 1 - core if across else core}
            return pltpu.make_async_remote_copy(
                src_ref=pieces.at[here], dst_ref=pieces.at[here], send_sem=rsend, recv_sem=rrecv,
                device_id=other)

        rest = [(a, i, j, k) for a in range(2) for i in range(RING) for j in range(RING) for k in range(RING)]
        for a, i, j, k in sorted(rest[1:], key=lambda o: -far(*o[1:])):
            tell(a, i, j, k).start()
        everyone = pieces.at[pl.ds(0, n_dev - 1)]
        pltpu.make_async_copy(everyone, everyone, rrecv).wait()
        ls = pieces[...].reshape(2 * RING, RING * RING, 128)
        peak = jnp.max(ls, axis=1, keepdims=True)
        mass = jnp.sum(jnp.exp(ls - peak), axis=1)
        whole = peak.reshape(2 * RING, 128) + jnp.log(mass)
        slot = lax.broadcasted_iota(jnp.int32, whole.shape, 1) % SLOT
        answer = jnp.where(slot >= 8, whole, 0.0)
        lane = lax.broadcasted_iota(jnp.int32, whole.shape, 1)
        answer = answer - jnp.where(lane == 0, jnp.sum(ls, axis=1), 0.0)
        answer = jnp.sum(jnp.sum(answer, axis=1, keepdims=True), axis=0, keepdims=True)
        group = lax.broadcasted_iota(jnp.int32, whole.shape, 0)
        losses = jnp.sum(jnp.where(group == core * RING + z, whole, 0.0), axis=0, keepdims=True)
        losses = losses - own
        spot = (y * RING + x) % 8 * SLOT + jnp.where(y >= 2, 8, 12)
        losses = pltpu.roll(jnp.broadcast_to(losses, (8, 128)), (128 - spot) % 128, 1)
        out_ref[0:1] = losses[0:1]
        out_ref[1:2] = jnp.broadcast_to(answer / (n_dev * n_q), (1, 128))

        for dy in range(RING):
            query_wait(dy, qsend)
        for way in range(2):
            for h in range(2):
                z_copy(way, h).wait_send()
            pass_copy(way).wait_send()
        swap_copy(0, 2).wait_send()
        for rel in OTHERS:
            for h in range(2):
                swap_copy(rel, h).wait_send()
        pltpu.make_async_copy(everyone, everyone, rsend).wait()

    return kernel


def hand_over(found_ref, loss_ref, mean_ref):
    loss_ref[...] = found_ref[0:1, :loss_ref.shape[1]]
    mean_ref[...] = found_ref[1:2, 0:1]


def solution(mesh):
    row_spec = P(('replica', 'data2', 'data'))
    tok_spec = P(('replica', 'data2', 'data'), None, None)
    mask_spec = P(('replica', 'data2', 'data'), None)

    def local_step(query_hidden, doc_hidden, w_proj, query_mask, doc_mask, temperature):
        n_q, qlen, hidden = query_hidden.shape
        n_docs, dlen, _ = doc_hidden.shape
        proj = w_proj.shape[1]
        chunks = n_q * qlen // SLOT
        dma = pltpu.SemaphoreType.DMA
        found = pl.pallas_call(
            make_kernel(n_docs, dlen, n_q, qlen),
            out_shape=jax.ShapeDtypeStruct((2, 128), jnp.float32),
            in_specs=[pl.BlockSpec(memory_space=pl.ANY)] * 6,
            out_specs=pl.BlockSpec(memory_space=pltpu.VMEM),
            scratch_shapes=[
                pltpu.VMEM(query_hidden.shape, jnp.bfloat16),
                pltpu.VMEM((dlen, n_docs, hidden), jnp.bfloat16),
                pltpu.VMEM(w_proj.shape, jnp.bfloat16),
                pltpu.VMEM(query_mask.shape, jnp.int32),
                pltpu.VMEM(doc_mask.shape, jnp.int32),
                pltpu.VMEM((1, 1), jnp.float32),
                pltpu.VMEM((chunks, RING, RING, SLOT, proj), jnp.bfloat16),
                pltpu.VMEM((RING, 2, n_docs * dlen, proj), jnp.bfloat16),
                pltpu.VMEM((RING, RING, 8, 128), jnp.float32),
                pltpu.VMEM((2 * RING ** 3, 1, 128), jnp.float32),
                dma((6,)),
                dma((4,)), dma((4,)),
                dma((2, 2)), dma((2, 2)),
                dma((2,)), dma((2,)),
                dma((RING, 2)), dma((RING, 2)),
                dma, dma,
            ],
            compiler_params=pltpu.CompilerParams(collective_id=0, has_side_effects=True),
        )(query_hidden, jnp.transpose(doc_hidden, (1, 0, 2)), w_proj, query_mask, doc_mask,
          temperature.reshape(1, 1))
        losses, mean = pl.pallas_call(
            hand_over,
            out_shape=(jax.ShapeDtypeStruct((1, n_q), jnp.float32),
                       jax.ShapeDtypeStruct((1, 1), jnp.float32)))(found)
        return losses.reshape(n_q), mean.reshape(1)

    return jax.shard_map(local_step, mesh=mesh,
                         in_specs=(tok_spec, tok_spec, P(None, None), mask_spec, mask_spec, P()),
                         out_specs=(row_spec, P('replica')), check_vma=False)
```

time: 34.6 us -> 32.6 us (0.942)
  Pallas kernels: 33.1 us -> 31.2 us
    pallas_call x1, Pallas kernels: 31.3 us -> 30 us  [local_step(): pl.pallas_call(make_kernel(n_docs, dlen, n_q, qlen), out_shape=jax.ShapeD...]
    pallas_call x1, Pallas kernels: 1.78 us -> 1.18 us  [local_step(): pl.pallas_call(hand_over, out_shape=(jax.ShapeDtypeStruct((1, n_q), jnp.f...]
where the time goes in v2:
time: 32.6 us; the launch traced here: 32.5 us
  Pallas kernels  31.2 us (96%)
  between operations  1.29 us (4%)
    pallas_call x1, Pallas kernels, local_step(): pl.pallas_call(make_kernel(n_docs, dlen, n_q, qlen), out_shape=jax.ShapeD...  30 us
    pallas_call x1, Pallas kernels, local_step(): pl.pallas_call(hand_over, out_shape=(jax.ShapeDtypeStruct((1, n_q), jnp.f...  1.18 us

profile of v2, /device:TPU:1, one launch (start us, length us, event | category | flops | bytes accessed | tf_op | source)
XLA Modules:
  0.0 32.5 jit_solution(9571334581208375474)
XLA Ops:
  1.3 30.0 %shard_map.77.found_ref = f32[2,128]{1,0:T(2,128)} custom-call(bf16[4,32,768]{2,1,0:T(8,128)(2,1)} %qh_hbm.1, bf16[180,4,768]{2,1,0:T(4,128)(2,1)} %bitcast.5, bf16[768,128]{1,0:T(8,128)(2,1)} %w_hbm.1, s32[4,32]{1,0:T(4,128)} %qm_hbm.1, s32[4,180]{1,0:T(4,128)} %dm_hbm.1, f32[1,1]{1,0:T(1,128)} %bitcast.4.temp_hbm), custom_call_target="tpu_custom_call" | custom-call | tf_op jit(solution)/shard_map/pallas_call | solution.py:316
  31.3 1.2 %shard_map.78 = (f32[1,4]{1,0:T(1,128)}, f32[1,1]{1,0:T(1,128)}) custom-call(f32[2,128]{1,0:T(2,128)} %shard_map.77.found_ref), custom_call_target="tpu_custom_call" | custom-call | tf_op jit(solution)/shard_map/pallas_call | solution.py:342

commit v3 on v2

--- a/solution.py
+++ b/solution.py
@@ -38,7 +38,7 @@
 
     def kernel(qh_hbm, dh_hbm, w_hbm, qm_hbm, dm_hbm, temp_hbm, out_ref,
                qh, dh, w, qm_ref, dm_ref, temp_ref, qbuf, pbuf, sums, pieces,
-               load_sem, qsend, qrecv, zsend, zrecv, fsend, frecv, dsend, drecv, rsend, rrecv):
+               load_sem, qsend, qrecv, zsend, zrecv, fsend, frecv, dsend, drecv, rsend, rrecv, ready):
         loads = [pltpu.make_async_copy(src, dst, load_sem.at[i]) for i, (src, dst) in enumerate((
             (w_hbm, w), (qh_hbm, qh), (qm_hbm, qm_ref), (dm_hbm, dm_ref), (dh_hbm, dh),
             (temp_hbm, temp_ref)))]
@@ -61,7 +61,7 @@
         barrier = pltpu.get_barrier_semaphore()
         mates = [(dy, dx) for dy in range(RING) for dx in range(RING) if dy or dx]
         mates.sort(key=lambda m: (far(m[0]), -far(m[1])))
-        near = [at(0, *m) for m in mates] + [sibling]
+        near = [at(0, 0, o) for o in OTHERS] + [at(0, o, 0) for o in OTHERS] + [sibling]
         near += [at(o, 0, 0) for o in OTHERS] + [at(o, 0, 0) | sibling for o in OTHERS]
         for device in near:
             pl.semaphore_signal(barrier, inc=1, device_id=device)
@@ -96,13 +96,6 @@
         def query_wait(dy, sem):
             ref = qbuf.at[:, (y + RING - dy) % RING, pl.ds(0, RING if dy else RING - 1)]
             pltpu.make_async_copy(ref, ref, sem.at[dy]).wait()
-
-        pl.semaphore_wait(barrier, len(near))
-        for near_row in (0, 1, 2):
-            for rnd in range(rounds):
-                for mate in mates:
-                    if far(mate[0]) == near_row:
-                        query_copy(mate, rnd).start()
 
         loads[3].wait()
         loads[4].wait()
@@ -146,10 +139,23 @@
                 src_ref=ref, dst_ref=ref, send_sem=fsend.at[way], recv_sem=frecv.at[way],
                 device_id=down if way else up)
 
+        pl.semaphore_wait(barrier, len(near))
+        for off in OTHERS:
+            pl.semaphore_signal(ready, inc=1, device_id=at(0, 0, off))
+        for rnd in range(rounds):
+            for mate in mates:
+                if 0 in mate:
+                    query_copy(mate, rnd).start()
         for i in range(2):
             for way in range(2):
                 z_copy(way, way ^ i).start()
         swap_copy(0, 2).start()
+        pl.semaphore_wait(ready, 3)
+        for near_row in (1, 2):
+            for rnd in range(rounds):
+                for mate in mates:
+                    if far(mate[0]) == near_row and mate[1]:
+                        query_copy(mate, rnd).start()
 
         sub = lax.broadcasted_iota(jnp.int32, (8, plane), 0)
         found, total = {}, {}
@@ -315,7 +321,7 @@
         dma = pltpu.SemaphoreType.DMA
         found = pl.pallas_call(
             make_kernel(n_docs, dlen, n_q, qlen),
-            out_shape=jax.ShapeDtypeStruct((2, 128), jnp.float32),
+            out_shape=pltpu.VMEM((2, 128), jnp.float32),
             in_specs=[pl.BlockSpec(memory_space=pl.ANY)] * 6,
             out_specs=pl.BlockSpec(memory_space=pltpu.VMEM),
             scratch_shapes=[
@@ -335,6 +341,7 @@
                 dma((2,)), dma((2,)),
                 dma((RING, 2)), dma((RING, 2)),
                 dma, dma,
+                pltpu.SemaphoreType.REGULAR,
             ],
             compiler_params=pltpu.CompilerParams(collective_id=0, has_side_effects=True),
         )(query_hidden, jnp.transpose(doc_hidden, (1, 0, 2)), w_proj, query_mask, doc_mask,
@@ -342,7 +349,10 @@
         losses, mean = pl.pallas_call(
             hand_over,
             out_shape=(jax.ShapeDtypeStruct((1, n_q), jnp.float32),
-                       jax.ShapeDtypeStruct((1, 1), jnp.float32)))(found)
+                       jax.ShapeDtypeStruct((1, 1), jnp.float32)),
+            in_specs=[pl.BlockSpec(memory_space=pltpu.VMEM)],
+            out_specs=(pl.BlockSpec(memory_space=pltpu.VMEM),) * 2,
+            compiler_params=pltpu.CompilerParams(vmem_limit_bytes=2 ** 20))(found)
         return losses.reshape(n_q), mean.reshape(1)
 
     return jax.shard_map(local_step, mesh=mesh,

time: 32.6 us -> 31.1 us (0.954)
  Pallas kernels: 31.2 us -> 29.6 us
    pallas_call x1, Pallas kernels: 30 us -> 29.1 us  [local_step(): pl.pallas_call(make_kernel(n_docs, dlen, n_q, qlen), out_shape=pltpu.VMEM...]
    pallas_call x1, Pallas kernels: 1.18 us -> 0.52 us  [local_step(): pl.pallas_call(hand_over, out_shape=(jax.ShapeDtypeStruct((1, n_q), jnp.f...]
where the time goes in v3:
time: 31.1 us; the launch traced here: 30.9 us
  Pallas kernels  29.6 us (95%)
  between operations  1.29 us (4%)
    pallas_call x1, Pallas kernels, local_step(): pl.pallas_call(make_kernel(n_docs, dlen, n_q, qlen), out_shape=pltpu.VMEM...  29.1 us

profile of v3, /device:TPU:1, one launch (start us, length us, event | category | flops | bytes accessed | tf_op | source)
XLA Modules:
  0.0 30.9 jit_solution(12799582219495384518)
XLA Ops:
  1.3 29.1 %shard_map.77.found_ref = f32[2,128]{1,0:T(2,128)S(1)} custom-call(bf16[4,32,768]{2,1,0:T(8,128)(2,1)} %qh_hbm.1, bf16[180,4,768]{2,1,0:T(4,128)(2,1)} %bitcast.5, bf16[768,128]{1,0:T(8,128)(2,1)} %w_hbm.1, s32[4,32]{1,0:T(4,128)} %qm_hbm.1, s32[4,180]{1,0:T(4,128)} %dm_hbm.1, f32[1,1]{1,0:T(1,128)} %bitcast.4.temp_hbm), custom_call_target="tpu_custom_call" | custom-call | tf_op jit(solution)/shard_map/pallas_call | solution.py:322
  30.4 0.5 %shard_map.78 = (f32[1,4]{1,0:T(1,128)}, f32[1,1]{1,0:T(1,128)}) custom-call(f32[2,128]{1,0:T(2,128)S(1)} %shard_map.77.found_ref), custom_call_target="tpu_custom_call" | custom-call | tf_op jit(solution)/shard_map/pallas_call | solution.py:349

commit v4 on v3

--- a/solution.py
+++ b/solution.py
@@ -59,7 +59,7 @@
         sibling = {'data2': 1 - core}
         up, down = at(1, 0, 0), at(RING - 1, 0, 0)
         barrier = pltpu.get_barrier_semaphore()
-        mates = [(dy, dx) for dy in range(RING) for dx in range(RING) if dy or dx]
+        mates = [(dy, dx) for dy in (0, 1, 3) for dx in range(RING) if dy or dx]
         mates.sort(key=lambda m: (far(m[0]), -far(m[1])))
         near = [at(0, 0, o) for o in OTHERS] + [at(0, o, 0) for o in OTHERS] + [sibling]
         near += [at(o, 0, 0) for o in OTHERS] + [at(o, 0, 0) | sibling for o in OTHERS]
@@ -89,13 +89,23 @@
 
         def query_copy(mate, rnd):
             ref = qbuf.at[pl.ds(rnd * (chunks // rounds), chunks // rounds), y, x]
-            return pltpu.make_async_remote_copy(
-                src_ref=ref, dst_ref=ref, send_sem=qsend.at[mate[0]], recv_sem=qrecv.at[mate[0]],
+            sem = mate[0], rnd * tiles // rounds
+            return pltpu.make_async_remote_copy(
+                src_ref=ref, dst_ref=ref, send_sem=qsend.at[sem], recv_sem=qrecv.at[sem],
                 device_id=at(0, *mate))
 
-        def query_wait(dy, sem):
-            ref = qbuf.at[:, (y + RING - dy) % RING, pl.ds(0, RING if dy else RING - 1)]
-            pltpu.make_async_copy(ref, ref, sem.at[dy]).wait()
+        def row_part(dy, t):
+            return qbuf.at[pl.ds(t * RING, RING), (y + RING - dy) % RING]
+
+        def query_wait(dy, t, sem):
+            ref = row_part(dy, t).at[:, pl.ds(0, RING if dy else RING - 1)]
+            pltpu.make_async_copy(ref, ref, sem.at[dy, t]).wait()
+
+        def row_copy(dy):
+            ref = row_part(dy, 0 if dy == 1 else 1)
+            return pltpu.make_async_remote_copy(
+                src_ref=ref, dst_ref=ref, send_sem=qsend.at[2, dy // 2], recv_sem=qrecv.at[2, dy // 2],
+                device_id=at(0, dy, 0))
 
         loads[3].wait()
         loads[4].wait()
@@ -110,7 +120,10 @@
         r = lax.broadcasted_iota(jnp.int32, keep.shape, 0)
         c = lax.broadcasted_iota(jnp.int32, keep.shape, 1)
         keep = jnp.sum(jnp.where(r % n_docs == c, keep, 0.0), axis=1, keepdims=True)
-        unit = unit_rows(dh[...].reshape(doc_rows, dh.shape[2]), w_val)
+        cut = dlen // 5
+        unit = jnp.concatenate([
+            unit_rows(dh[i:i + cut].reshape(cut * n_docs, dh.shape[2]), w[...])
+            for i in range(0, dlen, cut)], axis=0)
         unit = jnp.where(keep > 0, unit, 0.0).astype(jnp.bfloat16)
         valid = jnp.dot(pick, unit, preferred_element_type=jnp.float32)
         valid = jnp.concatenate([valid, valid], axis=0)
@@ -142,91 +155,96 @@
         pl.semaphore_wait(barrier, len(near))
         for off in OTHERS:
             pl.semaphore_signal(ready, inc=1, device_id=at(0, 0, off))
+        for i in range(2):
+            for way in range(2):
+                z_copy(way, way ^ i).start()
         for rnd in range(rounds):
             for mate in mates:
                 if 0 in mate:
                     query_copy(mate, rnd).start()
-        for i in range(2):
-            for way in range(2):
-                z_copy(way, way ^ i).start()
         swap_copy(0, 2).start()
         pl.semaphore_wait(ready, 3)
-        for near_row in (1, 2):
-            for rnd in range(rounds):
+        for i in range(tiles):
+            for rnd in range(rounds // tiles):
                 for mate in mates:
-                    if far(mate[0]) == near_row and mate[1]:
-                        query_copy(mate, rnd).start()
+                    if 0 not in mate:
+                        t = i if mate[0] == 1 else 1 - i
+                        query_copy(mate, t * (rounds // tiles) + rnd).start()
 
         sub = lax.broadcasted_iota(jnp.int32, (8, plane), 0)
         found, total = {}, {}
 
-        def score(rel, swapped, part, rows):
+        def score(rel, swapped, part, spots):
             docs = pbuf[(z + rel) % RING, 1 - core if swapped else core, parts[part]]
-            for dy in rows:
-                for t in range(tiles):
-                    q_tile = qbuf[t * RING:(t + 1) * RING, (y + RING - dy) % RING].reshape(plane, qbuf.shape[-1])
-                    sim = lax.dot_general(docs, q_tile, (((1,), (1,)), ((), ())),
-                                          preferred_element_type=jnp.float32)
-                    best = jnp.max(sim.reshape(docs.shape[0] // 8, 8, plane), axis=0)
-                    tile, key = (rel, swapped, dy, t), (rel, swapped, dy)
-                    if part < 2 and tile not in found:
-                        found[tile] = best
-                        continue
-                    if part < 2:
-                        best = jnp.maximum(best, found[tile])
-                    best = jnp.maximum(best, pltpu.roll(best, 4, 0))
-                    total[key] = total[key] + best if key in total else best
-
-        every, early = (0, 1, 2, 3), (0, 1)
-        query_wait(0, qrecv)
+            for dy, t in spots:
+                q_tile = row_part(dy, t)[...].reshape(plane, qbuf.shape[-1])
+                sim = lax.dot_general(docs, q_tile, (((1,), (1,)), ((), ())),
+                                      preferred_element_type=jnp.float32)
+                best = jnp.max(sim.reshape(docs.shape[0] // 8, 8, plane), axis=0)
+                tile, key = (rel, swapped, dy, t), (rel, swapped, dy)
+                if part < 2 and tile not in found:
+                    found[tile] = best
+                    continue
+                if part < 2:
+                    best = jnp.maximum(best, found[tile])
+                best = jnp.maximum(best, pltpu.roll(best, 4, 0))
+                total[key] = total[key] + best if key in total else best
+
+        sides, row0 = ((0, 3), (1, 1)), ((0, 0), (0, 1))
+        near0, near1, row2 = ((1, 0), (3, 1)), ((1, 1), (3, 0)), ((2, 0), (2, 1))
+        for t in range(tiles):
+            query_wait(0, t, qrecv)
         swap_copy(0, 2).wait_recv()
-        score(0, 0, 2, (0,))
-        score(0, 1, 2, (0,))
+        score(0, 0, 2, row0)
+        score(0, 1, 2, row0)
         for way in range(2):
             z_copy(way, way).wait_recv()
             pass_copy(way).start()
             swap_copy(1 if way else 3, way).start()
-        score(3, 0, 0, (0,))
-        score(1, 0, 1, (0,))
-        query_wait(1, qrecv)
-        score(0, 0, 2, (1,))
-        score(0, 1, 2, (1,))
-        score(3, 0, 0, (1,))
-        score(1, 0, 1, (1,))
+        for way, rel in sides:
+            score(rel, 0, way, row0)
         for way in range(2):
             z_copy(way, 1 - way).wait_recv()
             swap_copy(1 if way else 3, 1 - way).start()
         for way in range(2):
             swap_copy(1 if way else 3, way).wait_recv()
-        score(3, 1, 0, early)
-        score(1, 1, 1, early)
-        query_wait(3, qrecv)
-        score(0, 0, 2, (3,))
-        score(0, 1, 2, (3,))
-        score(3, 0, 0, (3,))
-        score(1, 0, 1, (3,))
-        score(3, 1, 0, (3,))
-        score(1, 1, 1, (3,))
-        score(3, 0, 1, (0, 1, 3))
-        score(1, 0, 0, (0, 1, 3))
+        for way, rel in sides:
+            score(rel, 0, 1 - way, row0)
+            score(rel, 1, way, row0)
+        query_wait(1, 0, qrecv)
+        row_copy(1).start()
+        query_wait(3, 1, qrecv)
+        row_copy(3).start()
+        for spots in (near0, near1):
+            if spots is near1:
+                query_wait(1, 1, qrecv)
+                query_wait(3, 0, qrecv)
+            score(0, 0, 2, spots)
+            score(0, 1, 2, spots)
+            for way, rel in sides:
+                score(rel, 0, way, spots)
+                score(rel, 1, way, spots)
+                score(rel, 0, 1 - way, spots)
         for way in range(2):
             pass_copy(way).wait_recv()
             swap_copy(2, way).start()
-        query_wait(2, qrecv)
         for way in range(2):
             swap_copy(1 if way else 3, 1 - way).wait_recv()
-        score(0, 0, 2, (2,))
-        score(0, 1, 2, (2,))
-        for way in range(2):
-            rel = 1 if way else 3
-            score(rel, 0, way, (2,))
-            score(rel, 1, way, (2,))
-            score(rel, 0, 1 - way, (2,))
-            score(rel, 1, 1 - way, every)
-        score(2, 0, 2, every)
+        for way, rel in sides:
+            score(rel, 1, 1 - way, row0 + near0 + near1)
+        score(2, 0, 2, row0 + near0 + near1)
+        row_copy(1).wait_recv()
+        row_copy(3).wait_recv()
         for h in range(2):
             swap_copy(2, h).wait_recv()
-        score(2, 1, 2, every)
+        score(0, 0, 2, row2)
+        score(0, 1, 2, row2)
+        for way, rel in sides:
+            for side in range(2):
+                score(rel, side, way, row2)
+                score(rel, side, 1 - way, row2)
+        score(2, 0, 2, row2)
+        score(2, 1, 2, row0 + near0 + near1 + row2)
 
         half = lax.broadcasted_iota(jnp.int32, (8, 128), 1) < 64
         for rel in range(RING):
@@ -288,8 +306,11 @@
         out_ref[0:1] = losses[0:1]
         out_ref[1:2] = jnp.broadcast_to(answer / (n_dev * n_q), (1, 128))
 
-        for dy in range(RING):
-            query_wait(dy, qsend)
+        for t in range(tiles):
+            for dy in (0, 1, 3):
+                query_wait(dy, t, qsend)
+        row_copy(1).wait_send()
+        row_copy(3).wait_send()
         for way in range(2):
             for h in range(2):
                 z_copy(way, h).wait_send()
@@ -336,7 +357,7 @@
                 pltpu.VMEM((RING, RING, 8, 128), jnp.float32),
                 pltpu.VMEM((2 * RING ** 3, 1, 128), jnp.float32),
                 dma((6,)),
-                dma((4,)), dma((4,)),
+                dma((RING, 2)), dma((RING, 2)),
                 dma((2, 2)), dma((2, 2)),
                 dma((2,)), dma((2,)),
                 dma((RING, 2)), dma((RING, 2)),

time: 31.1 us -> 30.1 us (0.968)
  Pallas kernels: 29.6 us -> 28.7 us
    pallas_call x1, Pallas kernels: 29.1 us -> 28.1 us  [local_step(): pl.pallas_call(make_kernel(n_docs, dlen, n_q, qlen), out_shape=pltpu.VMEM...]
where the time goes in v4:
time: 30.1 us; the launch traced here: 30 us
  Pallas kernels  28.7 us (95%)
  between operations  1.29 us (4%)
    pallas_call x1, Pallas kernels, local_step(): pl.pallas_call(make_kernel(n_docs, dlen, n_q, qlen), out_shape=pltpu.VMEM...  28.1 us

profile of v4, /device:TPU:1, one launch (start us, length us, event | category | flops | bytes accessed | tf_op | source)
XLA Modules:
  0.0 30.0 jit_solution(14690213204175205976)
XLA Ops:
  1.3 28.1 %shard_map.77.found_ref = f32[2,128]{1,0:T(2,128)S(1)} custom-call(bf16[4,32,768]{2,1,0:T(8,128)(2,1)} %qh_hbm.1, bf16[180,4,768]{2,1,0:T(4,128)(2,1)} %bitcast.5, bf16[768,128]{1,0:T(8,128)(2,1)} %w_hbm.1, s32[4,32]{1,0:T(4,128)} %qm_hbm.1, s32[4,180]{1,0:T(4,128)} %dm_hbm.1, f32[1,1]{1,0:T(1,128)} %bitcast.4.temp_hbm), custom_call_target="tpu_custom_call" | custom-call | tf_op jit(solution)/shard_map/pallas_call | solution.py:343
  29.4 0.5 %shard_map.78 = (f32[1,4]{1,0:T(1,128)}, f32[1,1]{1,0:T(1,128)}) custom-call(f32[2,128]{1,0:T(2,128)S(1)} %shard_map.77.found_ref), custom_call_target="tpu_custom_call" | custom-call | tf_op jit(solution)/shard_map/pallas_call | solution.py:370

commit v5 on v4

--- a/solution.py
+++ b/solution.py
@@ -8,6 +8,7 @@
 RING = 4
 SLOT = 16
 OTHERS = (1, 2, 3)
+ROW0, NEAR0, NEAR1, ROW2, SIDE0, SIDE1, PASSED, SWAP0, SWAP1, SWAP2 = 0, (1, 2), 3, 4, (5, 6), 7, 8, 9, (10, 11), 12
 
 
 def unit_rows(hidden, w):
@@ -38,7 +39,7 @@
 
     def kernel(qh_hbm, dh_hbm, w_hbm, qm_hbm, dm_hbm, temp_hbm, out_ref,
                qh, dh, w, qm_ref, dm_ref, temp_ref, qbuf, pbuf, sums, pieces,
-               load_sem, qsend, qrecv, zsend, zrecv, fsend, frecv, dsend, drecv, rsend, rrecv, ready):
+               sent, load_sem, send, recv, rsend, rrecv, ready):
         loads = [pltpu.make_async_copy(src, dst, load_sem.at[i]) for i, (src, dst) in enumerate((
             (w_hbm, w), (qh_hbm, qh), (qm_hbm, qm_ref), (dm_hbm, dm_ref), (dh_hbm, dh),
             (temp_hbm, temp_ref)))]
@@ -89,22 +90,21 @@
 
         def query_copy(mate, rnd):
             ref = qbuf.at[pl.ds(rnd * (chunks // rounds), chunks // rounds), y, x]
-            sem = mate[0], rnd * tiles // rounds
-            return pltpu.make_async_remote_copy(
-                src_ref=ref, dst_ref=ref, send_sem=qsend.at[sem], recv_sem=qrecv.at[sem],
-                device_id=at(0, *mate))
+            dy, t = mate[0], rnd * tiles // rounds
+            sem = ROW0 if dy == 0 else NEAR0[t] if t == dy // 2 else NEAR1
+            return pltpu.make_async_remote_copy(
+                src_ref=ref, dst_ref=ref, send_sem=send, recv_sem=recv.at[sem], device_id=at(0, *mate))
+
+        def arrived(sem, ref):
+            pltpu.make_async_copy(ref, ref, recv.at[sem]).wait()
 
         def row_part(dy, t):
             return qbuf.at[pl.ds(t * RING, RING), (y + RING - dy) % RING]
 
-        def query_wait(dy, t, sem):
-            ref = row_part(dy, t).at[:, pl.ds(0, RING if dy else RING - 1)]
-            pltpu.make_async_copy(ref, ref, sem.at[dy, t]).wait()
-
         def row_copy(dy):
             ref = row_part(dy, 0 if dy == 1 else 1)
             return pltpu.make_async_remote_copy(
-                src_ref=ref, dst_ref=ref, send_sem=qsend.at[2, dy // 2], recv_sem=qrecv.at[2, dy // 2],
+                src_ref=ref, dst_ref=ref, send_sem=send, recv_sem=recv.at[ROW2],
                 device_id=at(0, dy, 0))
 
         loads[3].wait()
@@ -136,22 +136,23 @@
 
         def swap_copy(rel, h):
             ref = doc_part(rel, h)
-            return pltpu.make_async_remote_copy(
-                src_ref=ref, dst_ref=ref, send_sem=dsend.at[rel, h % 2], recv_sem=drecv.at[rel, h % 2],
-                device_id=sibling)
+            sem = SWAP0 if rel == 0 else SWAP2 if rel == 2 else SWAP1[rel // 2 == h]
+            return pltpu.make_async_remote_copy(
+                src_ref=ref, dst_ref=ref, send_sem=send, recv_sem=recv.at[sem], device_id=sibling)
 
         def z_copy(way, h):
             ref = doc_part(0, h)
             return pltpu.make_async_remote_copy(
-                src_ref=ref, dst_ref=ref, send_sem=zsend.at[way, h], recv_sem=zrecv.at[way, h],
+                src_ref=ref, dst_ref=ref, send_sem=send, recv_sem=recv.at[SIDE0[way] if h == way else SIDE1],
                 device_id=down if way else up)
 
         def pass_copy(way):
             ref = doc_part(1 if way else RING - 1, way)
             return pltpu.make_async_remote_copy(
-                src_ref=ref, dst_ref=ref, send_sem=fsend.at[way], recv_sem=frecv.at[way],
+                src_ref=ref, dst_ref=ref, send_sem=send, recv_sem=recv.at[PASSED],
                 device_id=down if way else up)
 
+        loads[5].wait()
         pl.semaphore_wait(barrier, len(near))
         for off in OTHERS:
             pl.semaphore_signal(ready, inc=1, device_id=at(0, 0, off))
@@ -192,9 +193,9 @@
 
         sides, row0 = ((0, 3), (1, 1)), ((0, 0), (0, 1))
         near0, near1, row2 = ((1, 0), (3, 1)), ((1, 1), (3, 0)), ((2, 0), (2, 1))
-        for t in range(tiles):
-            query_wait(0, t, qrecv)
-        swap_copy(0, 2).wait_recv()
+        docs_ref, row_ref = pbuf.at[z, core], qbuf.at[:, y]
+        arrived(ROW0, row_ref.at[:, pl.ds(0, RING - 1)])
+        arrived(SWAP0, docs_ref)
         score(0, 0, 2, row0)
         score(0, 1, 2, row0)
         for way in range(2):
@@ -203,40 +204,35 @@
             swap_copy(1 if way else 3, way).start()
         for way, rel in sides:
             score(rel, 0, way, row0)
+        arrived(SIDE1, docs_ref)
         for way in range(2):
-            z_copy(way, 1 - way).wait_recv()
             swap_copy(1 if way else 3, 1 - way).start()
-        for way in range(2):
-            swap_copy(1 if way else 3, way).wait_recv()
+        arrived(SWAP1[0], docs_ref)
         for way, rel in sides:
             score(rel, 0, 1 - way, row0)
             score(rel, 1, way, row0)
-        query_wait(1, 0, qrecv)
+        arrived(NEAR0[0], row_part(1, 0))
         row_copy(1).start()
-        query_wait(3, 1, qrecv)
+        arrived(NEAR0[1], row_part(3, 1))
         row_copy(3).start()
         for spots in (near0, near1):
             if spots is near1:
-                query_wait(1, 1, qrecv)
-                query_wait(3, 0, qrecv)
+                arrived(NEAR1, row_ref)
             score(0, 0, 2, spots)
             score(0, 1, 2, spots)
             for way, rel in sides:
                 score(rel, 0, way, spots)
                 score(rel, 1, way, spots)
                 score(rel, 0, 1 - way, spots)
+        arrived(PASSED, docs_ref)
         for way in range(2):
-            pass_copy(way).wait_recv()
             swap_copy(2, way).start()
-        for way in range(2):
-            swap_copy(1 if way else 3, 1 - way).wait_recv()
+        arrived(SWAP1[1], docs_ref)
         for way, rel in sides:
             score(rel, 1, 1 - way, row0 + near0 + near1)
         score(2, 0, 2, row0 + near0 + near1)
-        row_copy(1).wait_recv()
-        row_copy(3).wait_recv()
-        for h in range(2):
-            swap_copy(2, h).wait_recv()
+        arrived(ROW2, row_ref)
+        arrived(SWAP2, docs_ref)
         score(0, 0, 2, row2)
         score(0, 1, 2, row2)
         for way, rel in sides:
@@ -252,7 +248,6 @@
                 s = jnp.where(sub < 4, total[rel, 0, dy], total[rel, 1, dy])
                 s = s[:, :128] + s[:, 128:]
                 sums[rel, (y + RING - dy) % RING] = s + pltpu.roll(s, 64, 1)
-        loads[5].wait()
         temp = temp_ref[...]
         logits = []
         for rel in range(RING):
@@ -285,7 +280,7 @@
                 device_id=other)
 
         rest = [(a, i, j, k) for a in range(2) for i in range(RING) for j in range(RING) for k in range(RING)]
-        for a, i, j, k in sorted(rest[1:], key=lambda o: -far(*o[1:])):
+        for a, i, j, k in sorted(rest[1:], key=lambda o: (-far(*o[1:]), -o[0])):
             tell(a, i, j, k).start()
         everyone = pieces.at[pl.ds(0, n_dev - 1)]
         pltpu.make_async_copy(everyone, everyone, rrecv).wait()
@@ -306,19 +301,7 @@
         out_ref[0:1] = losses[0:1]
         out_ref[1:2] = jnp.broadcast_to(answer / (n_dev * n_q), (1, 128))
 
-        for t in range(tiles):
-            for dy in (0, 1, 3):
-                query_wait(dy, t, qsend)
-        row_copy(1).wait_send()
-        row_copy(3).wait_send()
-        for way in range(2):
-            for h in range(2):
-                z_copy(way, h).wait_send()
-            pass_copy(way).wait_send()
-        swap_copy(0, 2).wait_send()
-        for rel in OTHERS:
-            for h in range(2):
-                swap_copy(rel, h).wait_send()
+        pltpu.make_async_copy(sent, sent, send).wait()
         pltpu.make_async_copy(everyone, everyone, rsend).wait()
 
     return kernel
@@ -339,6 +322,7 @@
         n_docs, dlen, _ = doc_hidden.shape
         proj = w_proj.shape[1]
         chunks = n_q * qlen // SLOT
+        sent_rows = (RING * (RING - 1) - 1 + RING) * n_q * qlen + 7 * n_docs * dlen
         dma = pltpu.SemaphoreType.DMA
         found = pl.pallas_call(
             make_kernel(n_docs, dlen, n_q, qlen),
@@ -356,12 +340,8 @@
                 pltpu.VMEM((RING, 2, n_docs * dlen, proj), jnp.bfloat16),
                 pltpu.VMEM((RING, RING, 8, 128), jnp.float32),
                 pltpu.VMEM((2 * RING ** 3, 1, 128), jnp.float32),
-                dma((6,)),
-                dma((RING, 2)), dma((RING, 2)),
-                dma((2, 2)), dma((2, 2)),
-                dma((2,)), dma((2,)),
-                dma((RING, 2)), dma((RING, 2)),
-                dma, dma,
+                pltpu.VMEM((sent_rows, proj), jnp.bfloat16),
+                dma((6,)), dma, dma((13,)), dma, dma,
                 pltpu.SemaphoreType.REGULAR,
             ],
             compiler_params=pltpu.CompilerParams(collective_id=0, has_side_effects=True),

time: 30.1 us -> 29.8 us (0.990)
    pallas_call x1, Pallas kernels: 28.1 us -> 27.8 us  [local_step(): pl.pallas_call(make_kernel(n_docs, dlen, n_q, qlen), out_shape=pltpu.VMEM...]
where the time goes in v5:
time: 29.8 us; the launch traced here: 29.6 us
  Pallas kernels  28.4 us (95%)
  between operations  1.29 us (4%)
    pallas_call x1, Pallas kernels, local_step(): pl.pallas_call(make_kernel(n_docs, dlen, n_q, qlen), out_shape=pltpu.VMEM...  27.8 us

profile of v5, /device:TPU:1, one launch (start us, length us, event | category | flops | bytes accessed | tf_op | source)
XLA Modules:
  0.0 29.6 jit_solution(14079835466776398368)
XLA Ops:
  1.3 27.8 %shard_map.77.found_ref = f32[2,128]{1,0:T(2,128)S(1)} custom-call(bf16[4,32,768]{2,1,0:T(8,128)(2,1)} %qh_hbm.1, bf16[180,4,768]{2,1,0:T(4,128)(2,1)} %bitcast.5, bf16[768,128]{1,0:T(8,128)(2,1)} %w_hbm.1, s32[4,32]{1,0:T(4,128)} %qm_hbm.1, s32[4,180]{1,0:T(4,128)} %dm_hbm.1, f32[1,1]{1,0:T(1,128)} %bitcast.4.temp_hbm), custom_call_target="tpu_custom_call" | custom-call | tf_op jit(solution)/shard_map/pallas_call | solution.py:327
  29.1 0.5 %shard_map.78 = (f32[1,4]{1,0:T(1,128)}, f32[1,1]{1,0:T(1,128)}) custom-call(f32[2,128]{1,0:T(2,128)S(1)} %shard_map.77.found_ref), custom_call_target="tpu_custom_call" | custom-call | tf_op jit(solution)/shard_map/pallas_call | solution.py:350

commit v6 on v5

--- a/solution.py
+++ b/solution.py
@@ -8,7 +8,7 @@
 RING = 4
 SLOT = 16
 OTHERS = (1, 2, 3)
-ROW0, NEAR0, NEAR1, ROW2, SIDE0, SIDE1, PASSED, SWAP0, SWAP1, SWAP2 = 0, (1, 2), 3, 4, (5, 6), 7, 8, 9, (10, 11), 12
+ROW0, NEAR0, NEAR1, ROW2, SIDE0, SIDE1, PASSED, SWAP0, SWAP1, SWAP2 = 0, (1, 2), 3, 4, (5, 6, 13, 14), 7, 8, 9, (10, 11), 12
 
 
 def unit_rows(hidden, w):
@@ -30,7 +30,9 @@
 def make_kernel(n_docs, dlen, n_q, qlen):
     doc_rows = n_docs * dlen
     head = doc_rows // 2 // 16 * 16 + 16
+    cuts = (0, head // 32 * 16 + 16, head, head + (doc_rows - head) // 32 * 16, doc_rows)
     parts = (pl.ds(0, head), pl.ds(head, doc_rows - head), pl.ds(0, doc_rows))
+    parts += tuple(pl.ds(a, b - a) for a, b in zip(cuts, cuts[1:]))
     chunks = n_q * qlen // SLOT
     tiles = chunks // RING
     rounds = 4
@@ -39,7 +41,7 @@
 
     def kernel(qh_hbm, dh_hbm, w_hbm, qm_hbm, dm_hbm, temp_hbm, out_ref,
                qh, dh, w, qm_ref, dm_ref, temp_ref, qbuf, pbuf, sums, pieces,
-               sent, load_sem, send, recv, rsend, rrecv, ready):
+               sent, q_rows_ref, load_sem, send, recv, rsend, rrecv, ready):
         loads = [pltpu.make_async_copy(src, dst, load_sem.at[i]) for i, (src, dst) in enumerate((
             (w_hbm, w), (qh_hbm, qh), (qm_hbm, qm_ref), (dm_hbm, dm_ref), (dh_hbm, dh),
             (temp_hbm, temp_ref)))]
@@ -68,9 +70,6 @@
             pl.semaphore_signal(barrier, inc=1, device_id=device)
 
         q_rows = n_q * qlen
-        r = lax.broadcasted_iota(jnp.int32, (q_rows, q_rows), 0)
-        c = lax.broadcasted_iota(jnp.int32, (q_rows, q_rows), 1)
-        order = jnp.where(c == (r % n_q) * qlen + r // n_q, 1.0, 0.0).astype(jnp.bfloat16)
         r = lax.broadcasted_iota(jnp.int32, (doc_rows, dlen), 0)
         c = lax.broadcasted_iota(jnp.int32, (doc_rows, dlen), 1)
         spread = jnp.where(r // n_docs == c, 1.0, 0.0).astype(jnp.bfloat16)
@@ -82,11 +81,10 @@
         loads[1].wait()
         w_val = w[...]
         q_unit = unit_rows(qh[...].reshape(q_rows, qh.shape[2]), w_val)
-        q_vec = jnp.where(q_keep > 0, q_unit, 0.0).astype(jnp.bfloat16)
-        q_ord = jnp.dot(order, q_vec, preferred_element_type=jnp.float32).astype(jnp.bfloat16)
-        q_ord = q_ord.reshape(chunks, SLOT, q_ord.shape[1])
+        q_rows_ref[...] = jnp.where(q_keep > 0, q_unit, 0.0)
         for k in range(chunks):
-            qbuf[k, y, x] = q_ord[k]
+            block = [q_rows_ref[pl.ds(k * (SLOT // n_q) + t, n_q, stride=qlen)] for t in range(SLOT // n_q)]
+            qbuf[k, y, x] = jnp.concatenate(block, axis=0).astype(jnp.bfloat16)
 
         def query_copy(mate, rnd):
             ref = qbuf.at[pl.ds(rnd * (chunks // rounds), chunks // rounds), y, x]
@@ -142,12 +140,13 @@
 
         def z_copy(way, h):
             ref = doc_part(0, h)
-            return pltpu.make_async_remote_copy(
-                src_ref=ref, dst_ref=ref, send_sem=send, recv_sem=recv.at[SIDE0[way] if h == way else SIDE1],
+            sem = SIDE1 if h < 2 else SIDE0[h - 3]
+            return pltpu.make_async_remote_copy(
+                src_ref=ref, dst_ref=ref, send_sem=send, recv_sem=recv.at[sem],
                 device_id=down if way else up)
 
-        def pass_copy(way):
-            ref = doc_part(1 if way else RING - 1, way)
+        def pass_copy(way, i):
+            ref = doc_part(1 if way else RING - 1, 3 + 2 * way + i)
             return pltpu.make_async_remote_copy(
                 src_ref=ref, dst_ref=ref, send_sem=send, recv_sem=recv.at[PASSED],
                 device_id=down if way else up)
@@ -156,9 +155,9 @@
         pl.semaphore_wait(barrier, len(near))
         for off in OTHERS:
             pl.semaphore_signal(ready, inc=1, device_id=at(0, 0, off))
-        for i in range(2):
+        for i in range(3):
             for way in range(2):
-                z_copy(way, way ^ i).start()
+                z_copy(way, 1 - way if i == 2 else 3 + 2 * way + i).start()
         for rnd in range(rounds):
             for mate in mates:
                 if 0 in mate:
@@ -198,23 +197,25 @@
         arrived(SWAP0, docs_ref)
         score(0, 0, 2, row0)
         score(0, 1, 2, row0)
-        for way in range(2):
-            z_copy(way, way).wait_recv()
-            pass_copy(way).start()
-            swap_copy(1 if way else 3, way).start()
+        for i in range(2):
+            for way in range(2):
+                z_copy(way, 3 + 2 * way + i).wait_recv()
+                pass_copy(way, i).start()
+                if i:
+                    swap_copy(1 if way else 3, way).start()
         for way, rel in sides:
             score(rel, 0, way, row0)
         arrived(SIDE1, docs_ref)
         for way in range(2):
             swap_copy(1 if way else 3, 1 - way).start()
         arrived(SWAP1[0], docs_ref)
-        for way, rel in sides:
-            score(rel, 0, 1 - way, row0)
-            score(rel, 1, way, row0)
         arrived(NEAR0[0], row_part(1, 0))
         row_copy(1).start()
         arrived(NEAR0[1], row_part(3, 1))
         row_copy(3).start()
+        for way, rel in sides:
+            score(rel, 0, 1 - way, row0)
+            score(rel, 1, way, row0)
         for spots in (near0, near1):
             if spots is near1:
                 arrived(NEAR1, row_ref)
@@ -341,7 +342,8 @@
                 pltpu.VMEM((RING, RING, 8, 128), jnp.float32),
                 pltpu.VMEM((2 * RING ** 3, 1, 128), jnp.float32),
                 pltpu.VMEM((sent_rows, proj), jnp.bfloat16),
-                dma((6,)), dma, dma((13,)), dma, dma,
+                pltpu.VMEM((n_q * qlen, proj), jnp.float32),
+                dma((6,)), dma, dma((15,)), dma, dma,
                 pltpu.SemaphoreType.REGULAR,
             ],
             compiler_params=pltpu.CompilerParams(collective_id=0, has_side_effects=True),

time: 29.8 us -> 29.6 us (level)
  no operation moved by 1% of the time
where the time goes in v6:
time: 29.6 us; the launch traced here: 29.5 us
  Pallas kernels  28.2 us (95%)
  between operations  1.29 us (4%)
    pallas_call x1, Pallas kernels, local_step(): pl.pallas_call(make_kernel(n_docs, dlen, n_q, qlen), out_shape=pltpu.VMEM...  27.7 us

profile of v6, /device:TPU:1, one launch (start us, length us, event | category | flops | bytes accessed | tf_op | source)
XLA Modules:
  0.0 29.5 jit_solution(6056650619003752489)
XLA Ops:
  1.3 27.7 %shard_map.77.found_ref = f32[2,128]{1,0:T(2,128)S(1)} custom-call(bf16[4,32,768]{2,1,0:T(8,128)(2,1)} %qh_hbm.1, bf16[180,4,768]{2,1,0:T(4,128)(2,1)} %bitcast.5, bf16[768,128]{1,0:T(8,128)(2,1)} %w_hbm.1, s32[4,32]{1,0:T(4,128)} %qm_hbm.1, s32[4,180]{1,0:T(4,128)} %dm_hbm.1, f32[1,1]{1,0:T(1,128)} %bitcast.4.temp_hbm), custom_call_target="tpu_custom_call" | custom-call | tf_op jit(solution)/shard_map/pallas_call | solution.py:328
  29.0 0.5 %shard_map.78 = (f32[1,4]{1,0:T(1,128)}, f32[1,1]{1,0:T(1,128)}) custom-call(f32[2,128]{1,0:T(2,128)S(1)} %shard_map.77.found_ref), custom_call_target="tpu_custom_call" | custom-call | tf_op jit(solution)/shard_map/pallas_call | solution.py:352

commit v7 on v6

--- a/solution.py
+++ b/solution.py
@@ -43,10 +43,10 @@
                qh, dh, w, qm_ref, dm_ref, temp_ref, qbuf, pbuf, sums, pieces,
                sent, q_rows_ref, load_sem, send, recv, rsend, rrecv, ready):
         loads = [pltpu.make_async_copy(src, dst, load_sem.at[i]) for i, (src, dst) in enumerate((
-            (w_hbm, w), (qh_hbm, qh), (qm_hbm, qm_ref), (dm_hbm, dm_ref), (dh_hbm, dh),
-            (temp_hbm, temp_ref)))]
-        for load in loads:
-            load.start()
+            (w_hbm, w), (qh_hbm, qh), (qm_hbm, qm_ref), (dm_hbm, dm_ref), (dh_hbm.at[pl.ds(0, 108)], dh.at[pl.ds(0, 108)]),
+            (temp_hbm, temp_ref), (dh_hbm.at[pl.ds(108, 72)], dh.at[pl.ds(108, 72)])))]
+        for i, load in enumerate(loads):
+            load.start(priority=1 if i in (4, 6) else 0)
 
         core = lax.axis_index('data2')
         me = lax.axis_index('data')
@@ -107,6 +107,7 @@
 
         loads[3].wait()
         loads[4].wait()
+        loads[6].wait()
         dm = dm_ref[...].astype(jnp.float32)
         lane = lax.broadcasted_iota(jnp.int32, dm.shape, 1)
         first = jnp.min(jnp.where(dm > 0, lane, dlen), axis=1, keepdims=True)
@@ -343,7 +344,7 @@
                 pltpu.VMEM((2 * RING ** 3, 1, 128), jnp.float32),
                 pltpu.VMEM((sent_rows, proj), jnp.bfloat16),
                 pltpu.VMEM((n_q * qlen, proj), jnp.float32),
-                dma((6,)), dma, dma((15,)), dma, dma,
+                dma((7,)), dma, dma((15,)), dma, dma,
                 pltpu.SemaphoreType.REGULAR,
             ],
             compiler_params=pltpu.CompilerParams(collective_id=0, has_side_effects=True),

time: 29.6 us -> 29.6 us (level)
  no operation moved by 1% of the time
where the time goes in v7:
time: 29.6 us; the launch traced here: 29.4 us
  Pallas kernels  28.1 us (95%)
  between operations  1.29 us (4%)
    pallas_call x1, Pallas kernels, local_step(): pl.pallas_call(make_kernel(n_docs, dlen, n_q, qlen), out_shape=pltpu.VMEM...  27.6 us

profile of v7, /device:TPU:1, one launch (start us, length us, event | category | flops | bytes accessed | tf_op | source)
XLA Modules:
  0.0 29.4 jit_solution(11553836650651452745)
XLA Ops:
  1.3 27.6 %shard_map.77.found_ref = f32[2,128]{1,0:T(2,128)S(1)} custom-call(bf16[4,32,768]{2,1,0:T(8,128)(2,1)} %qh_hbm.1, bf16[180,4,768]{2,1,0:T(4,128)(2,1)} %bitcast.5, bf16[768,128]{1,0:T(8,128)(2,1)} %w_hbm.1, s32[4,32]{1,0:T(4,128)} %qm_hbm.1, s32[4,180]{1,0:T(4,128)} %dm_hbm.1, f32[1,1]{1,0:T(1,128)} %bitcast.4.temp_hbm), custom_call_target="tpu_custom_call" | custom-call | tf_op jit(solution)/shard_map/pallas_call | solution.py:329
  28.9 0.5 %shard_map.78 = (f32[1,4]{1,0:T(1,128)}, f32[1,1]{1,0:T(1,128)}) custom-call(f32[2,128]{1,0:T(2,128)S(1)} %shard_map.77.found_ref), custom_call_target="tpu_custom_call" | custom-call | tf_op jit(solution)/shard_map/pallas_call | solution.py:353

commit v8 on v7

--- a/solution.py
+++ b/solution.py
@@ -42,7 +42,7 @@
     def kernel(qh_hbm, dh_hbm, w_hbm, qm_hbm, dm_hbm, temp_hbm, out_ref,
                qh, dh, w, qm_ref, dm_ref, temp_ref, qbuf, pbuf, sums, pieces,
                sent, q_rows_ref, load_sem, send, recv, rsend, rrecv, ready):
-        loads = [pltpu.make_async_copy(src, dst, load_sem.at[i]) for i, (src, dst) in enumerate((
+        loads = [pltpu.make_async_copy(src, dst, load_sem.at[(0, 0, 2, 3, 4, 1, 4)[i]]) for i, (src, dst) in enumerate((
             (w_hbm, w), (qh_hbm, qh), (qm_hbm, qm_ref), (dm_hbm, dm_ref), (dh_hbm.at[pl.ds(0, 108)], dh.at[pl.ds(0, 108)]),
             (temp_hbm, temp_ref), (dh_hbm.at[pl.ds(108, 72)], dh.at[pl.ds(108, 72)])))]
         for i, load in enumerate(loads):
@@ -77,8 +77,8 @@
         qm = qm_ref[...].astype(jnp.float32)
         q_keep = jnp.concatenate([as_column(qm[i:i + 1], qlen) for i in range(n_q)], axis=0)
 
-        loads[0].wait()
-        loads[1].wait()
+        both = sent.at[pl.ds(0, w.shape[0] + n_q * qlen * qh.shape[2] // w.shape[1])]
+        pltpu.make_async_copy(both, both, load_sem.at[0]).wait()
         w_val = w[...]
         q_unit = unit_rows(qh[...].reshape(q_rows, qh.shape[2]), w_val)
         q_rows_ref[...] = jnp.where(q_keep > 0, q_unit, 0.0)
@@ -106,8 +106,7 @@
                 device_id=at(0, dy, 0))
 
         loads[3].wait()
-        loads[4].wait()
-        loads[6].wait()
+        pltpu.make_async_copy(dh_hbm, dh, load_sem.at[4]).wait()
         dm = dm_ref[...].astype(jnp.float32)
         lane = lax.broadcasted_iota(jnp.int32, dm.shape, 1)
         first = jnp.min(jnp.where(dm > 0, lane, dlen), axis=1, keepdims=True)
@@ -344,7 +343,7 @@
                 pltpu.VMEM((2 * RING ** 3, 1, 128), jnp.float32),
                 pltpu.VMEM((sent_rows, proj), jnp.bfloat16),
                 pltpu.VMEM((n_q * qlen, proj), jnp.float32),
-                dma((7,)), dma, dma((15,)), dma, dma,
+                dma((5,)), dma, dma((15,)), dma, dma,
                 pltpu.SemaphoreType.REGULAR,
             ],
             compiler_params=pltpu.CompilerParams(collective_id=0, has_side_effects=True),

time: 29.6 us -> 29.5 us (level)
  no operation moved by 1% of the time
where the time goes in v8:
time: 29.5 us; the launch traced here: 29.4 us
  Pallas kernels  28.1 us (95%)
  between operations  1.29 us (4%)
    pallas_call x1, Pallas kernels, local_step(): pl.pallas_call(make_kernel(n_docs, dlen, n_q, qlen), out_shape=pltpu.VMEM...  27.6 us

profile of v8, /device:TPU:1, one launch (start us, length us, event | category | flops | bytes accessed | tf_op | source)
XLA Modules:
  0.0 29.4 jit_solution(10007373042546701947)
XLA Ops:
  1.3 27.6 %shard_map.77.found_ref = f32[2,128]{1,0:T(2,128)S(1)} custom-call(bf16[4,32,768]{2,1,0:T(8,128)(2,1)} %qh_hbm.1, bf16[180,4,768]{2,1,0:T(4,128)(2,1)} %bitcast.5, bf16[768,128]{1,0:T(8,128)(2,1)} %w_hbm.1, s32[4,32]{1,0:T(4,128)} %qm_hbm.1, s32[4,180]{1,0:T(4,128)} %dm_hbm.1, f32[1,1]{1,0:T(1,128)} %bitcast.4.temp_hbm), custom_call_target="tpu_custom_call" | custom-call | tf_op jit(solution)/shard_map/pallas_call | solution.py:328
  28.9 0.5 %shard_map.78 = (f32[1,4]{1,0:T(1,128)}, f32[1,1]{1,0:T(1,128)}) custom-call(f32[2,128]{1,0:T(2,128)S(1)} %shard_map.77.found_ref), custom_call_target="tpu_custom_call" | custom-call | tf_op jit(solution)/shard_map/pallas_call | solution.py:352
